TPU v7x, 32 devices: a whole 2x2x4 slice. The times are simulated.
32 devices in a mesh: row: 8 (over z, x), col: 4 (over y, core).
Axes of the slice: x: 2, y: 2, z: 4, core: 2. Of those that a mesh axis runs over, the one named last changes fastest.
Arguments:
- p_values: bfloat16 [96, 512, 128], P('row', 'col'), may hold values from -0.8984375 to 0.8984375
- p_where: int32 [96, 8], P('row', 'col'), may hold values from 0 to 63, as said below
- p_count: int32 [8, 4], P('row', 'col'), may hold values from 6 to 12, as said below
- h_values: bfloat16 [96, 512, 128], P('row', 'col'), may hold values from -3 to 3
- h_where: int32 [96, 8], P('row', 'col'), may hold values from 0 to 63, as said below
- h_count: int32 [8, 4], P('row', 'col'), may hold values from 6 to 12, as said below
Outputs:
- ph_values: bfloat16 [96, 512, 128], P('row', 'col')
- php_values: bfloat16 [96, 512, 128], P('row', 'col')
- energy: float32 [], replicated
Inputs may be any that keep to these rules, and one draw needn't show every extreme that they name: `p_where`: the 12 slots of the device of row index i and column index j name distinct blocks of its own tile: block rows i * 8 to i * 8 + 7 and the j-th of 4 equal ranges of block columns. `h_where`: as for p_where. `p_count`: some device has all 12 slots live. `h_count`: some device has all 12 slots live.
All inputs are finite; a program needn't handle non-finite values.
Results may differ from a plain program's by a relative error of at most 0.0049.
Values may be sent and summed in bfloat16 or wider, within the bound.
A program may use at most 64 MiB of HBM per device.

v0:
```python
import jax
import jax.numpy as jnp
from jax import lax
from jax.sharding import PartitionSpec as P

TILE = 8


def contribute(total_sum, left_tile, right_tile, band_index, out_where):
    left_vals, left_where, left_count = left_tile
    right_vals, right_where, right_count = right_tile
    slot_count = left_vals.shape[0]
    inner_blocks = band_index * TILE + jnp.arange(TILE, dtype=jnp.int32)
    left_live = jnp.arange(slot_count, dtype=jnp.int32) < left_count[0, 0]
    right_live = jnp.arange(slot_count, dtype=jnp.int32) < right_count[0, 0]
    match_left = (
        (left_where[None, None, :, 0] == out_where[:, None, None, 0])
        & (left_where[None, None, :, 1] == inner_blocks[None, :, None])
        & left_live[None, None, :]
    )
    match_right = (
        (right_where[None, None, :, 1] == out_where[:, None, None, 1])
        & (right_where[None, None, :, 0] == inner_blocks[None, :, None])
        & right_live[None, None, :]
    )
    pick_left = jnp.argmax(match_left.astype(jnp.int32), axis=2)
    pick_right = jnp.argmax(match_right.astype(jnp.int32), axis=2)
    has_left = jnp.any(match_left, axis=2)
    has_right = jnp.any(match_right, axis=2)
    nothing = jnp.zeros((), jnp.bfloat16)

    def slot_product(items):
        left_pick, left_has, right_pick, right_has = items
        row_blocks = jnp.where(left_has[:, None, None], left_vals[left_pick], nothing)
        col_blocks = jnp.where(right_has[:, None, None], right_vals[right_pick], nothing)
        return jnp.einsum("kxy,kyz->xz", row_blocks, col_blocks, preferred_element_type=jnp.float32)

    return total_sum + lax.map(slot_product, (pick_left, has_left, pick_right, has_right))


def pick_tile(gathered, owner, slot_count):
    all_vals, all_where, all_count = gathered
    start = (owner * slot_count).astype(jnp.int32)
    vals = lax.dynamic_slice_in_dim(all_vals, start, slot_count, 0)
    where = lax.dynamic_slice_in_dim(all_where, start, slot_count, 0)
    count = lax.dynamic_slice_in_dim(all_count, owner.astype(jnp.int32), 1, 0)
    return (vals, where, count)


def multiply(left_tile, right_tile, out_where):
    rows_count = lax.axis_size("row")
    cols_count = lax.axis_size("col")
    band_ratio = rows_count // cols_count
    slot_count = out_where.shape[0]
    block_size = left_tile[0].shape[1]
    zero_sum = jnp.zeros((slot_count, block_size, block_size), jnp.float32)
    left_all = (
        lax.all_gather(left_tile[0], "col", axis=0, tiled=True),
        lax.all_gather(left_tile[1], "col", axis=0, tiled=True),
        lax.all_gather(left_tile[2], "col", axis=0, tiled=True),
    )
    right_all = (
        lax.all_gather(right_tile[0], "row", axis=0, tiled=True),
        lax.all_gather(right_tile[1], "row", axis=0, tiled=True),
        lax.all_gather(right_tile[2], "row", axis=0, tiled=True),
    )

    def band_step(band_index, total_sum):
        left_here = pick_tile(left_all, band_index // band_ratio, slot_count)
        right_here = pick_tile(right_all, band_index, slot_count)
        return contribute(total_sum, left_here, right_here, band_index, out_where)

    return lax.fori_loop(0, rows_count, band_step, zero_sum)


def per_device(p_values, p_where, p_count, h_values, h_where, h_count):
    slot_count = p_values.shape[0]
    live_slots = jnp.arange(slot_count, dtype=jnp.int32) < p_count[0, 0]
    density_tile = (p_values, p_where, p_count)
    first_sum = multiply(density_tile, (h_values, h_where, h_count), p_where)
    first_sum = jnp.where(live_slots[:, None, None], first_sum, jnp.float32(0.0))
    traces = jnp.trace(first_sum, axis1=1, axis2=2)
    diagonal = live_slots & (p_where[:, 0] == p_where[:, 1])
    local_energy = jnp.sum(jnp.where(diagonal, traces, jnp.float32(0.0)))
    ph_values = first_sum.astype(jnp.bfloat16)
    second_sum = multiply((ph_values, p_where, p_count), density_tile, p_where)
    php_values = jnp.where(live_slots[:, None, None], second_sum, jnp.float32(0.0)).astype(
        jnp.bfloat16
    )
    energy = lax.psum(local_energy, ("row", "col"))
    return (ph_values, php_values, energy)


def solution(mesh):
    placed = (
        P("row", "col", None),
        P("row", "col"),
        P("row", "col"),
        P("row", "col", None),
        P("row", "col"),
        P("row", "col"),
    )
    return jax.shard_map(
        per_device,
        mesh=mesh,
        in_specs=placed,
        out_specs=(P("row", "col", None), P("row", "col", None), P()),
        check_vma=False,
    )
```

profile of v0, /device:TPU:0, one launch (start us, length us, event | category | flops | bytes accessed | tf_op | source)
XLA Modules:
  0.0 582.8 jit_solution(3601513037107337282)
XLA Ops:
  10.1 1.2 dynamic-slice.1
  11.3 1.2 dynamic-slice
  13.9 6.4 %all-reduce = s32[4]{0:T(128)S(1)} all-reduce(s32[4]{0:T(128)S(1)} %bitcast_dynamic-update-slice_fusion.2), channel_id=1, replica_groups=mesh['row'=8,'col'=4] {'col'}, use_global_device_ids=true, to_apply=%add | all-reduce | flops 4 | bytes 32
  20.4 5.4 all-gather
  25.9 21.1 %all-gather.1 = s32[8,12,2]{1,2,0:T(2,128)S(1)} all-gather(s32[1,12,2]{1,2,0:T(2,128)} %bitcast.156), channel_id=1, replica_groups=mesh['row'=8,'col'=4] {'row'}, dimensions={0}, use_global_device_ids=true | all-gather | bytes 864 | tf_op jit(solution)/shard_map/all_gather | solution.py:64
  48.4 7.2 %all-reduce.3 = (s32[8]{0:T(128)S(1)}, s32[8]{0:T(128)S(1)}) all-reduce(s32[8]{0:T(128)S(1)} %bitcast_dynamic-update-slice_fusion, s32[8]{0:T(128)S(1)} %bitcast_dynamic-update-slice_fusion.1), channel_id=1, replica_groups=mesh['row'=8,'col'=4] {'row'}, use_global_device_ids=true, to_apply=%add.1 | all-reduce | flops 16 | bytes 128
  55.6 38.7 %all-gather.10.cloned.1.call-done = bf16[96,128,128]{2,1,0:T(8,128)(2,1)} async-done(((bf16[12,128,128]{2,1,0:T(8,128)(2,1)}), bf16[96,128,128]{2,1,0:T(8,128)(2,1)}) %all-gather.10.cloned.1.call-update) | async-done | bytes 3145744 | tf_op jit(solution)/shard_map/all_gather | solution.py:63
  94.3 211.2 %while.103 = (s32[]{:T(128)}, f32[12,128,128]{2,1,0:T(8,128)S(1)}, s32[48,2]{0,1:T(2,128)S(1)}, s32[12,2]{0,1:T(2,128)}, s32[4,1]{0,1:T(1,128)S(1)}, /*index=5*/...) while((s32[]{:T(128)}, f32[12,128,128]{2,1,0:T(8,128)S(1)}, ...), condition=%wide.region_7.8_spmd.clone.clone, body=%wide.region_0.7_spmd.clone.sunk.clone | while | flops 34240836 | bytes 5585244 | solution.py:73
  94.3 1.2 constant_dynamic-slice_fusion.30
  97.7 1.1 iota_reduce_fusion.12
  99.6 1.1 iota_reduce_fusion.13
  101.3 19.1 %while.102 = (s32[]{:T(128)}, f32[12,128,128]{2,1,0:T(8,128)S(1)}, pred[12,8]{1,0:T(8,128)(4,1)S(1)}, s32[12,8]{1,0:T(8,128)S(1)}, bf16[12,128,128]{2,1,0:T(8,12...) while((s32[]{:T(128)}, f32[12,128,128]{2,1,0:T(8,128)S(1)}, ...), condition=%wide.region_6.6_spmd, body=%wide.region_5.5_spmd.sunk | while | flops 33818672 | bytes 1648009 | solution.py:38
  120.7 1.2 constant_dynamic-slice_fusion.30
  124.1 1.1 iota_reduce_fusion.12
  126.0 1.1 iota_reduce_fusion.13
  127.7 19.1 %while.102 = (s32[]{:T(128)}, f32[12,128,128]{2,1,0:T(8,128)S(1)}, pred[12,8]{1,0:T(8,128)(4,1)S(1)}, s32[12,8]{1,0:T(8,128)S(1)}, bf16[12,128,128]{2,1,0:T(8,12...) while((s32[]{:T(128)}, f32[12,128,128]{2,1,0:T(8,128)S(1)}, ...), condition=%wide.region_6.6_spmd, body=%wide.region_5.5_spmd.sunk | while | flops 33818672 | bytes 1648009 | solution.py:38
  147.1 1.2 constant_dynamic-slice_fusion.30
  152.4 1.1 iota_reduce_fusion.13
  154.1 19.1 %while.102 = (s32[]{:T(128)}, f32[12,128,128]{2,1,0:T(8,128)S(1)}, pred[12,8]{1,0:T(8,128)(4,1)S(1)}, s32[12,8]{1,0:T(8,128)S(1)}, bf16[12,128,128]{2,1,0:T(8,12...) while((s32[]{:T(128)}, f32[12,128,128]{2,1,0:T(8,128)S(1)}, ...), condition=%wide.region_6.6_spmd, body=%wide.region_5.5_spmd.sunk | while | flops 33818672 | bytes 1648009 | solution.py:38
  173.5 1.2 constant_dynamic-slice_fusion.30
  176.9 1.1 iota_reduce_fusion.12
  178.8 1.1 iota_reduce_fusion.13
  180.5 19.1 %while.102 = (s32[]{:T(128)}, f32[12,128,128]{2,1,0:T(8,128)S(1)}, pred[12,8]{1,0:T(8,128)(4,1)S(1)}, s32[12,8]{1,0:T(8,128)S(1)}, bf16[12,128,128]{2,1,0:T(8,12...) while((s32[]{:T(128)}, f32[12,128,128]{2,1,0:T(8,128)S(1)}, ...), condition=%wide.region_6.6_spmd, body=%wide.region_5.5_spmd.sunk | while | flops 33818672 | bytes 1648009 | solution.py:38
  199.9 1.2 constant_dynamic-slice_fusion.30
  203.4 1.1 iota_reduce_fusion.12
  206.9 19.1 %while.102 = (s32[]{:T(128)}, f32[12,128,128]{2,1,0:T(8,128)S(1)}, pred[12,8]{1,0:T(8,128)(4,1)S(1)}, s32[12,8]{1,0:T(8,128)S(1)}, bf16[12,128,128]{2,1,0:T(8,12...) while((s32[]{:T(128)}, f32[12,128,128]{2,1,0:T(8,128)S(1)}, ...), condition=%wide.region_6.6_spmd, body=%wide.region_5.5_spmd.sunk | while | flops 33818672 | bytes 1648009 | solution.py:38
  226.3 1.2 constant_dynamic-slice_fusion.30
  229.8 1.1 iota_reduce_fusion.12
  233.3 19.1 %while.102 = (s32[]{:T(128)}, f32[12,128,128]{2,1,0:T(8,128)S(1)}, pred[12,8]{1,0:T(8,128)(4,1)S(1)}, s32[12,8]{1,0:T(8,128)S(1)}, bf16[12,128,128]{2,1,0:T(8,12...) while((s32[]{:T(128)}, f32[12,128,128]{2,1,0:T(8,128)S(1)}, ...), condition=%wide.region_6.6_spmd, body=%wide.region_5.5_spmd.sunk | while | flops 33818672 | bytes 1648009 | solution.py:38
  252.8 1.2 constant_dynamic-slice_fusion.30
  256.2 1.1 iota_reduce_fusion.12
  259.7 19.1 %while.102 = (s32[]{:T(128)}, f32[12,128,128]{2,1,0:T(8,128)S(1)}, pred[12,8]{1,0:T(8,128)(4,1)S(1)}, s32[12,8]{1,0:T(8,128)S(1)}, bf16[12,128,128]{2,1,0:T(8,12...) while((s32[]{:T(128)}, f32[12,128,128]{2,1,0:T(8,128)S(1)}, ...), condition=%wide.region_6.6_spmd, body=%wide.region_5.5_spmd.sunk | while | flops 33818672 | bytes 1648009 | solution.py:38
  279.2 1.2 constant_dynamic-slice_fusion.30
  282.6 1.1 iota_reduce_fusion.12
  286.2 19.1 %while.102 = (s32[]{:T(128)}, f32[12,128,128]{2,1,0:T(8,128)S(1)}, pred[12,8]{1,0:T(8,128)(4,1)S(1)}, s32[12,8]{1,0:T(8,128)S(1)}, bf16[12,128,128]{2,1,0:T(8,12...) while((s32[]{:T(128)}, f32[12,128,128]{2,1,0:T(8,128)S(1)}, ...), condition=%wide.region_6.6_spmd, body=%wide.region_5.5_spmd.sunk | while | flops 33818672 | bytes 1648009 | solution.py:38
  306.5 18.5 %all-gather.2 = s32[8,12,2]{1,2,0:T(2,128)S(1)} all-gather(s32[1,12,2]{1,2,0:T(2,128)} %bitcast.152), channel_id=1, replica_groups=mesh['row'=8,'col'=4] {'row'}, dimensions={0}, use_global_device_ids=true | all-gather | bytes 864 | tf_op jit(solution)/shard_map/all_gather | solution.py:64
  325.3 1.4 fusion.27
  326.7 37.0 %psum.7 = f32[]{:T(128)} all-reduce(f32[]{:T(128)} %fusion.27), channel_id=1, replica_groups=mesh['row'=8,'col'=4] {'row','col'}, use_global_device_ids=true, to_apply=%region_18.19 | all-reduce | flops 1 | bytes 8 | tf_op jit(solution)/shard_map/psum | solution.py:90
  363.7 211.7 %while.105 = (s32[]{:T(128)}, f32[12,128,128]{2,1,0:T(8,128)S(1)}, s32[48,2]{0,1:T(2,128)S(1)}, s32[12,2]{0,1:T(2,128)}, s32[4,1]{0,1:T(1,128)S(1)}, /*index=5*/...) while((s32[]{:T(128)}, f32[12,128,128]{2,1,0:T(8,128)S(1)}, ...), condition=%wide.region_15.16_spmd.clone.clone, body=%wide.region_8.15_spmd.clone.sunk.clone | while | flops 34240836 | bytes 5585244 | solution.py:73
  363.7 1.2 constant_dynamic-slice_fusion.33
  367.2 1.1 iota_reduce_fusion.14
  369.1 1.1 iota_reduce_fusion.15
  370.8 19.1 %while.104 = (s32[]{:T(128)}, f32[12,128,128]{2,1,0:T(8,128)S(1)}, pred[12,8]{1,0:T(8,128)(4,1)S(1)}, s32[12,8]{1,0:T(8,128)S(1)}, bf16[12,128,128]{2,1,0:T(8,12...) while((s32[]{:T(128)}, f32[12,128,128]{2,1,0:T(8,128)S(1)}, ...), condition=%wide.region_14.14_spmd, body=%wide.region_13.13_spmd.sunk | while | flops 33818672 | bytes 1648009 | solution.py:38
  390.2 1.2 constant_dynamic-slice_fusion.33
  393.7 1.1 iota_reduce_fusion.14
  395.5 1.1 iota_reduce_fusion.15
  397.3 19.1 %while.104 = (s32[]{:T(128)}, f32[12,128,128]{2,1,0:T(8,128)S(1)}, pred[12,8]{1,0:T(8,128)(4,1)S(1)}, s32[12,8]{1,0:T(8,128)S(1)}, bf16[12,128,128]{2,1,0:T(8,12...) while((s32[]{:T(128)}, f32[12,128,128]{2,1,0:T(8,128)S(1)}, ...), condition=%wide.region_14.14_spmd, body=%wide.region_13.13_spmd.sunk | while | flops 33818672 | bytes 1648009 | solution.py:38
  416.7 1.2 constant_dynamic-slice_fusion.33
  423.7 19.1 %while.104 = (s32[]{:T(128)}, f32[12,128,128]{2,1,0:T(8,128)S(1)}, pred[12,8]{1,0:T(8,128)(4,1)S(1)}, s32[12,8]{1,0:T(8,128)S(1)}, bf16[12,128,128]{2,1,0:T(8,12...) while((s32[]{:T(128)}, f32[12,128,128]{2,1,0:T(8,128)S(1)}, ...), condition=%wide.region_14.14_spmd, body=%wide.region_13.13_spmd.sunk | while | flops 33818672 | bytes 1648009 | solution.py:38
  443.1 1.2 constant_dynamic-slice_fusion.33
  446.6 1.1 iota_reduce_fusion.14
  448.5 1.1 iota_reduce_fusion.15
  450.2 19.1 %while.104 = (s32[]{:T(128)}, f32[12,128,128]{2,1,0:T(8,128)S(1)}, pred[12,8]{1,0:T(8,128)(4,1)S(1)}, s32[12,8]{1,0:T(8,128)S(1)}, bf16[12,128,128]{2,1,0:T(8,12...) while((s32[]{:T(128)}, f32[12,128,128]{2,1,0:T(8,128)S(1)}, ...), condition=%wide.region_14.14_spmd, body=%wide.region_13.13_spmd.sunk | while | flops 33818672 | bytes 1648009 | solution.py:38
  469.6 1.2 constant_dynamic-slice_fusion.33
  474.9 1.1 iota_reduce_fusion.15
  476.6 19.1 %while.104 = (s32[]{:T(128)}, f32[12,128,128]{2,1,0:T(8,128)S(1)}, pred[12,8]{1,0:T(8,128)(4,1)S(1)}, s32[12,8]{1,0:T(8,128)S(1)}, bf16[12,128,128]{2,1,0:T(8,12...) while((s32[]{:T(128)}, f32[12,128,128]{2,1,0:T(8,128)S(1)}, ...), condition=%wide.region_14.14_spmd, body=%wide.region_13.13_spmd.sunk | while | flops 33818672 | bytes 1648009 | solution.py:38
  496.0 1.2 constant_dynamic-slice_fusion.33
  503.1 19.1 %while.104 = (s32[]{:T(128)}, f32[12,128,128]{2,1,0:T(8,128)S(1)}, pred[12,8]{1,0:T(8,128)(4,1)S(1)}, s32[12,8]{1,0:T(8,128)S(1)}, bf16[12,128,128]{2,1,0:T(8,12...) while((s32[]{:T(128)}, f32[12,128,128]{2,1,0:T(8,128)S(1)}, ...), condition=%wide.region_14.14_spmd, body=%wide.region_13.13_spmd.sunk | while | flops 33818672 | bytes 1648009 | solution.py:38
  522.5 1.2 constant_dynamic-slice_fusion.33
  526.0 1.1 iota_reduce_fusion.14
  527.8 1.1 iota_reduce_fusion.15
  529.6 19.1 %while.104 = (s32[]{:T(128)}, f32[12,128,128]{2,1,0:T(8,128)S(1)}, pred[12,8]{1,0:T(8,128)(4,1)S(1)}, s32[12,8]{1,0:T(8,128)S(1)}, bf16[12,128,128]{2,1,0:T(8,12...) while((s32[]{:T(128)}, f32[12,128,128]{2,1,0:T(8,128)S(1)}, ...), condition=%wide.region_14.14_spmd, body=%wide.region_13.13_spmd.sunk | while | flops 33818672 | bytes 1648009 | solution.py:38
  549.0 1.2 constant_dynamic-slice_fusion.33
  556.0 19.1 %while.104 = (s32[]{:T(128)}, f32[12,128,128]{2,1,0:T(8,128)S(1)}, pred[12,8]{1,0:T(8,128)(4,1)S(1)}, s32[12,8]{1,0:T(8,128)S(1)}, bf16[12,128,128]{2,1,0:T(8,12...) while((s32[]{:T(128)}, f32[12,128,128]{2,1,0:T(8,128)S(1)}, ...), condition=%wide.region_14.14_spmd, body=%wide.region_13.13_spmd.sunk | while | flops 33818672 | bytes 1648009 | solution.py:38
  (1626 shorter events, 373.5 us)
Async XLA Ops:
  7.2 48.5 %all-gather.8.cloned.1.call-start = ((), (), s32[]{:S(2)}) async-start(), calls=%async_computation | async-start | bytes 1966080 | tf_op jit(solution)/shard_map/all_gather | solution.py:58
  7.9 86.4 %all-gather.10.cloned.1.call-start = ((), (), s32[]{:S(2)}) async-start(), calls=%async_computation.1 | async-start | bytes 3538944 | tf_op jit(solution)/shard_map/all_gather | solution.py:63
  8.6 355.1 %all-gather.14.cloned.1.call-start = ((), (), s32[]{:S(2)}) async-start(), calls=%async_computation.3 | async-start | bytes 3538944 | tf_op jit(solution)/shard_map/all_gather | solution.py:63
  9.4 354.3 %all-gather.12.cloned.1.call-start = ((), (), s32[]{:S(2)}) async-start(), calls=%async_computation.2 | async-start | bytes 1966080 | tf_op jit(solution)/shard_map/all_gather | solution.py:58
Sparse Core Ops, SparseCore 0:
  9.5 22.3 all-gather.7
  34.1 60.1 all-gather.9
  96.5 58.7 all-gather.13
  306.6 18.3 all-gather.11
where the time goes:
time: 585 us; the launch traced here: 583 us
  local copies, waits for them, and re-layouts  279 us (48%)
  blocking collectives  95.7 us (16%)
  other arithmetic  81.8 us (14%)
  matrix products  55.1 us (9%)
  waiting for transfers between devices  40.8 us (7%)
  between operations  15.2 us (3%)
  loops' own time  14.8 us (3%)
    gather x192, local copies, waits for them, and re-layouts, slot_product(): right_vals[right_pick]  115 us
    gather x192, local copies, waits for them, and re-layouts, slot_product(): left_vals[left_pick]  115 us
    dot_general x192, matrix products, slot_product(): jnp.einsum('kxy,kyz->xz', row_blocks, col_blocks, preferred_element_type=...  55.1 us
    all_gather x2, blocking collectives, multiply(): lax.all_gather(right_tile[1], 'row', axis=0, tiled=True)  39.6 us
    all_gather x2, waiting for transfers between devices, multiply(): lax.all_gather(right_tile[0], 'row', axis=0, tiled=True)  38.7 us
    psum x1, blocking collectives, per_device(): energy = lax.psum(local_energy, ('row', 'col'))  37 us
    another operation x32, other arithmetic, contribute(): pick_left = jnp.argmax(match_left.astype(jnp.int32), axis=2)  35.9 us
    dynamic_slice x16, local copies, waits for them, and re-layouts, pick_tile(): vals = lax.dynamic_slice_in_dim(all_vals, start, slot_count, 0)  18.7 us
  transfers between devices with their start and end apart: 4, of which 1 were waited for; matrix products, arithmetic and copies ran while one was open for 36% of the time, Pallas kernels for 0%

commit v1 on v0

v1 whole, which is shorter than its diff:
```python
import functools

import jax
import jax.numpy as jnp
from jax import lax
from jax.experimental import pallas as pl
from jax.experimental.pallas import tpu as pltpu
from jax.sharding import PartitionSpec as P

TILE = 8
CHUNKS = 3
IN_FLIGHT = 16
MESH = pl.DeviceIdType.MESH
ANY = pl.BlockSpec(memory_space=pl.ANY)
VMEM = pl.BlockSpec(memory_space=pltpu.VMEM)
SMEM = pl.BlockSpec(memory_space=pltpu.SMEM)


def at_row(r):
    return (r, lax.axis_index("col"))


def at_col(c):
    return (lax.axis_index("row"), c)


def remote(src, dst, send_sem, recv_sem, device):
    return pltpu.make_async_remote_copy(
        src_ref=src,
        dst_ref=dst,
        send_sem=send_sem,
        recv_sem=recv_sem,
        device_id=device,
        device_id_type=MESH,
    )


def greet(rows, cols):
    me_row, me_col = lax.axis_index("row"), lax.axis_index("col")
    barrier = pltpu.get_barrier_semaphore()
    for d in range(1, rows):
        pl.semaphore_signal(
            barrier, inc=1, device_id=at_row((me_row + d) % rows), device_id_type=MESH
        )
    for d in range(1, cols):
        pl.semaphore_signal(
            barrier, inc=1, device_id=at_col((me_col + d) % cols), device_id_type=MESH
        )
    pl.semaphore_wait(barrier, rows + cols - 2)


class ColumnGather:
    def __init__(self, rows, own, out, own_send, own_recv, fwd_send):
        self.rows, self.own, self.out = rows, own, out
        self.sems = own_send, own_recv, fwd_send
        self.inner = 2 if rows % 2 == 0 else 1
        self.outer = rows // self.inner
        slots = own.shape[0]
        self.chunks = CHUNKS if slots % CHUNKS == 0 else 1
        self.size = slots // self.chunks
        self.me = lax.axis_index("row")
        self.x, self.z = self.me % self.inner, self.me // self.inner
        self.pair = self.z * self.inner + (self.inner - 1 - self.x)

    def row_of(self, d):
        return ((self.z + d) % self.outer) * self.inner + self.x

    def part(self, ch):
        return pl.ds(ch * self.size, self.size)

    def send(self, ch, d):
        own_send, recv, _ = self.sems
        target = self.pair if d == 0 else self.row_of(d)
        return remote(
            self.own.at[self.part(ch)],
            self.out.at[self.me, self.part(ch)],
            own_send.at[d, ch],
            recv.at[self.me, ch],
            at_row(target),
        )

    def forward(self, ch, d):
        _, recv, fwd = self.sems
        r = self.row_of(d)
        return remote(
            self.out.at[r, self.part(ch)],
            self.out.at[r, self.part(ch)],
            fwd.at[d, ch],
            recv.at[r, ch],
            at_row(self.pair),
        )

    def arrival(self, ch, r):
        _, recv, fwd = self.sems
        return remote(
            self.out.at[r, self.part(ch)],
            self.out.at[r, self.part(ch)],
            fwd.at[0, ch],
            recv.at[r, ch],
            at_row(self.pair),
        )

    def order(self):
        out = []
        for k in range(1, self.outer):
            d = (k + 1) // 2 if k % 2 else -(k // 2)
            out.append(d % self.outer)
        return out

    def start(self):
        for ch in range(self.chunks):
            if self.inner == 2:
                self.send(ch, 0).start()
            for d in self.order():
                self.send(ch, d).start()

    def relay(self, ch):
        for d in self.order():
            self.arrival(ch, self.row_of(d)).wait_recv()
            if self.inner == 2:
                self.forward(ch, d).start()

    def finish(self):
        for ch in range(self.chunks):
            if self.inner == 2:
                self.arrival(ch, self.pair).wait_recv()
                self.send(ch, 0).wait_send()
            for d in self.order():
                self.send(ch, d).wait_send()
                if self.inner == 2:
                    other = ((self.z + d) % self.outer) * self.inner + (1 - self.x)
                    self.arrival(ch, other).wait_recv()
                    self.forward(ch, d).wait_send()


def col_copies(cols, own, out, send, recv):
    me = lax.axis_index("col")
    made = []
    for d in range(1, cols):
        made.append(
            remote(own, out.at[me], send.at[d], recv.at[d], at_col((me + d) % cols))
        )
    return made


def row_copies(rows, own, out, send, recv):
    me = lax.axis_index("row")
    made = []
    for d in range(1, rows):
        made.append(
            remote(own, out.at[me], send.at[d], recv.at[d], at_row((me + d) % rows))
        )
    return made


def first_gather(
    rows, cols, p_ref, h_ref, meta_ref, prow, hcol, prow_meta, col_meta,
    own_send, own_recv, fwd_send, p_send, p_recv, mc_send, mc_recv, mr_send, mr_recv, local,
):
    me_row, me_col = lax.axis_index("row"), lax.axis_index("col")
    keep = [
        pltpu.make_async_copy(h_ref, hcol.at[me_row], local.at[0]),
        pltpu.make_async_copy(p_ref, prow.at[me_col], local.at[1]),
        pltpu.make_async_copy(meta_ref, prow_meta.at[me_col], local.at[2]),
        pltpu.make_async_copy(meta_ref, col_meta.at[me_row], local.at[3]),
    ]
    greet(rows, cols)
    gather = ColumnGather(rows, h_ref, hcol, own_send, own_recv, fwd_send)
    gather.start()
    across = (
        col_copies(cols, p_ref, prow, p_send, p_recv)
        + col_copies(cols, meta_ref, prow_meta, mc_send, mc_recv)
        + row_copies(rows, meta_ref, col_meta, mr_send, mr_recv)
    )
    for copy in across + keep:
        copy.start()
    for ch in range(gather.chunks):
        gather.relay(ch)
    gather.finish()
    for copy in across + keep:
        copy.wait()


def second_gather(
    rows, cols, p_ref, f_ref, e_ref, frow, pcol, e_out,
    e_cols, e_rows, e_sum,
    own_send, own_recv, fwd_send, p_send, p_recv, ec_send, ec_recv, er_send, er_recv, local,
):
    me_row, me_col = lax.axis_index("row"), lax.axis_index("col")
    keep = [
        pltpu.make_async_copy(p_ref, pcol.at[me_row], local.at[0]),
        pltpu.make_async_copy(f_ref, frow.at[me_col], local.at[1]),
    ]
    greet(rows, cols)
    energies = col_copies(cols, e_ref, e_cols, ec_send, ec_recv)
    for copy in energies:
        copy.start()
    gather = ColumnGather(rows, p_ref, pcol, own_send, own_recv, fwd_send)
    gather.start()
    across = col_copies(cols, f_ref, frow, p_send, p_recv)
    for copy in across + keep:
        copy.start()
    e_cols[me_col] = e_ref[...]
    for copy in energies:
        copy.wait()
    total = e_cols[0]
    for c in range(1, cols):
        total = total + e_cols[c]
    e_sum[...] = total
    e_rows[me_row] = total
    gather.relay(0)
    sums = row_copies(rows, e_sum, e_rows, er_send, er_recv)
    for copy in sums:
        copy.start()
    for ch in range(1, gather.chunks):
        gather.relay(ch)
    for copy in sums:
        copy.wait()
    total = e_rows[0]
    for r in range(1, rows):
        total = total + e_rows[r]
    e_out[...] = total
    gather.finish()
    for copy in across + keep:
        copy.wait()


def block_products(
    rows, cols, right_lane, with_trace, lmeta, rmeta, left, right, *rest
):
    if with_trace:
        out, e_out = rest[:2]
    else:
        e_in, out, e_out = rest[:3]
    acc, lbuf, rbuf, head, nxt, inner, mask, table, ml, mr, ms, sems = rest[-12:]
    slots = out.shape[0]
    i, j = lax.axis_index("row"), lax.axis_index("col")
    nblk = rows * TILE
    tile_cols = nblk // cols
    words = -(-nblk // 32)
    count_lane = 4 * slots
    acc[...] = jnp.zeros_like(acc)

    for t in range(TILE):
        head[t] = -1

    for t in range(tile_cols * words):
        mask[t] = 0

    @pl.loop(0, cols)
    def _(c):
        @pl.loop(0, lmeta[c, 0, count_lane])
        def _(s):
            row = lmeta[c, 0, s] - i * TILE
            idx = c * slots + s
            inner[idx] = lmeta[c, 0, slots + s]
            nxt[idx] = head[row]
            head[row] = idx

    @pl.loop(0, rows)
    def _(r):
        @pl.loop(0, rmeta[r, 0, count_lane + (1 if right_lane else 0)])
        def _(s):
            k = rmeta[r, 0, right_lane + s]
            col = rmeta[r, 0, right_lane + slots + s] - j * tile_cols
            word = col * words + (k >> 5)
            mask[word] = mask[word] | (jnp.int32(1) << (k & 31))
            table[k * tile_cols + col] = r * slots + s

    def find_slot(s, n):
        row = lmeta[j, 0, s] - i * TILE
        col = lmeta[j, 0, slots + s] - j * tile_cols

        def more(state):
            return state[0] >= 0

        def step(state):
            at, n = state
            k = inner[at]
            ml[n] = at
            mr[n] = table[k * tile_cols + col]
            ms[n] = s
            return nxt[at], n + ((mask[col * words + (k >> 5)] >> (k & 31)) & 1)

        return lax.while_loop(more, step, (head[row], n))[1]

    own_count = lmeta[j, 0, count_lane]
    found = lax.fori_loop(0, own_count, find_slot, jnp.int32(0))

    def fetch(base, m):
        a, b = ml[base + m], mr[base + m]
        return (
            pltpu.make_async_copy(left.at[a], lbuf.at[m], sems.at[0, m]),
            pltpu.make_async_copy(right.at[b], rbuf.at[m], sems.at[1, m]),
        )

    @pl.loop(0, (found + IN_FLIGHT - 1) // IN_FLIGHT)
    def _(chunk):
        base = chunk * IN_FLIGHT
        size = jnp.minimum(found - base, IN_FLIGHT)

        @pl.loop(0, size)
        def _(m):
            for copy in fetch(base, m):
                copy.start()

        @pl.loop(0, size)
        def _(m):
            for copy in fetch(base, m):
                copy.wait()
            s = ms[base + m]
            acc[s] += jnp.dot(lbuf[m], rbuf[m], preferred_element_type=jnp.float32)

    out[...] = acc[...].astype(out.dtype)
    if with_trace:
        size = acc.shape[1]
        e_out[...] = jnp.zeros_like(e_out)
        diagonal = lax.broadcasted_iota(jnp.int32, (size, size), 0) == lax.broadcasted_iota(
            jnp.int32, (size, size), 1
        )

        @pl.loop(0, own_count)
        def _(s):
            @pl.when(lmeta[j, 0, s] == lmeta[j, 0, slots + s])
            def _():
                e_out[...] += jnp.sum(jnp.where(diagonal, acc[s], 0.0))
    else:
        e_out[0, 0] = e_in[0, 0]


def per_device(rows, cols, p_values, p_where, p_count, h_values, h_where, h_count):
    slots, size, _ = p_values.shape
    dtype = p_values.dtype
    nblk = rows * TILE
    tile_cols = nblk // cols
    words = -(-nblk // 32)
    meta = jnp.concatenate(
        [p_where[:, 0], p_where[:, 1], h_where[:, 0], h_where[:, 1], p_count[0], h_count[0]]
    )
    meta = jnp.broadcast_to(jnp.pad(meta, (0, 128 - meta.shape[0]))[None, :], (8, 128))
    dma = pltpu.SemaphoreType.DMA
    chunk_sems = [dma((rows, CHUNKS)), dma((rows, CHUNKS)), dma((rows, CHUNKS))]
    col_sems = [dma((cols,)), dma((cols,))]
    row_sems = [dma((rows,)), dma((rows,))]
    tile = (slots, size, size)
    prow, hcol, prow_meta, col_meta = pl.pallas_call(
        functools.partial(first_gather, rows, cols),
        out_shape=[
            jax.ShapeDtypeStruct((cols,) + tile, dtype),
            jax.ShapeDtypeStruct((rows,) + tile, dtype),
            jax.ShapeDtypeStruct((cols, 8, 128), jnp.int32),
            jax.ShapeDtypeStruct((rows, 8, 128), jnp.int32),
        ],
        in_specs=[VMEM] * 3,
        out_specs=[ANY] * 4,
        scratch_shapes=chunk_sems + col_sems + col_sems + row_sems + [dma((4,))],
        compiler_params=pltpu.CompilerParams(collective_id=0, has_side_effects=True),
        name="first_gather",
    )(p_values, h_values, meta)

    def products(right_lane, with_trace, lmeta, rmeta, left, right, *more):
        smem = lambda n: pltpu.SMEM((n,), jnp.int32)
        most = slots * nblk + 1
        return pl.pallas_call(
            functools.partial(block_products, rows, cols, right_lane, with_trace),
            out_shape=[
                jax.ShapeDtypeStruct(tile, dtype),
                jax.ShapeDtypeStruct((8, 128) if with_trace else (1, 1), jnp.float32),
            ],
            in_specs=[SMEM, SMEM, ANY, ANY] + [SMEM] * len(more),
            out_specs=[VMEM, VMEM if with_trace else SMEM],
            scratch_shapes=[
                pltpu.VMEM(tile, jnp.float32),
                pltpu.VMEM((IN_FLIGHT, size, size), dtype),
                pltpu.VMEM((IN_FLIGHT, size, size), dtype),
                smem(TILE),
                smem(cols * slots),
                smem(cols * slots),
                smem(tile_cols * words),
                smem(nblk * tile_cols),
                smem(most),
                smem(most),
                smem(most),
                dma((2, IN_FLIGHT)),
            ],
            name="products",
        )(
            lmeta,
            rmeta,
            left.reshape((cols * slots, size, size)),
            right.reshape((rows * slots, size, size)),
            *more,
        )

    ph_values, part = products(2 * slots, True, prow_meta, col_meta, prow, hcol)
    frow, pcol, energy = pl.pallas_call(
        functools.partial(second_gather, rows, cols),
        out_shape=[
            jax.ShapeDtypeStruct((cols,) + tile, dtype),
            jax.ShapeDtypeStruct((rows,) + tile, dtype),
            jax.ShapeDtypeStruct((8, 128), jnp.float32),
        ],
        in_specs=[VMEM] * 3,
        out_specs=[ANY, ANY, VMEM],
        scratch_shapes=[
            pltpu.VMEM((cols, 8, 128), jnp.float32),
            pltpu.VMEM((rows, 8, 128), jnp.float32),
            pltpu.VMEM((8, 128), jnp.float32),
        ]
        + chunk_sems + col_sems + col_sems + row_sems + [dma((2,))],
        compiler_params=pltpu.CompilerParams(collective_id=1, has_side_effects=True),
        name="second_gather",
    )(p_values, ph_values, part)
    php_values, energy = products(0, False, prow_meta, col_meta, frow, pcol, energy)
    return (ph_values, php_values, energy[0, 0])


def solution(mesh):
    placed = (
        P("row", "col", None),
        P("row", "col"),
        P("row", "col"),
        P("row", "col", None),
        P("row", "col"),
        P("row", "col"),
    )
    return jax.shard_map(
        functools.partial(per_device, mesh.shape["row"], mesh.shape["col"]),
        mesh=mesh,
        in_specs=placed,
        out_specs=(P("row", "col", None), P("row", "col", None), P()),
        check_vma=False,
    )
```

time: 585 us -> 114 us (0.19)
  local copies, waits for them, and re-layouts: 279 us -> 1.45 us
  Pallas kernels: 0 us -> 109 us
  blocking collectives: 95.7 us -> 0 us
  other arithmetic: 81.8 us -> 0 us
  matrix products: 55.1 us -> 0 us
  waiting for transfers between devices: 40.8 us -> 0 us
  loops' own time: 14.8 us -> 0 us
  between operations: 15.2 us -> 1.95 us
    gather x384 -> x0, local copies, waits for them, and re-layouts: 229 us -> none  [the longest x192 115 us: slot_product(): right_vals[right_pick]]
    pallas_call x0 -> x4, Pallas kernels: none -> 109 us  [the longest x1 50.7 us: per_device(): pl.pallas_call(functools.partial(first_gather, rows, cols), out_shape=[ja...]
    dot_general x192 -> x0, matrix products: 55.1 us -> none  [slot_product(): jnp.einsum('kxy,kyz->xz', row_blocks, col_blocks, preferred_element_type=...]
    all_gather x3 -> x0, blocking collectives: 45 us -> none  [the longest x2 39.6 us: multiply(): lax.all_gather(right_tile[1], 'row', axis=0, tiled=True)]
    all_gather x4 -> x0, waiting for transfers between devices: 38.7 us -> none  [the longest x2 38.7 us: multiply(): lax.all_gather(right_tile[0], 'row', axis=0, tiled=True)]
    psum x1 -> x0, blocking collectives: 37 us -> none  [per_device(): energy = lax.psum(local_energy, ('row', 'col'))]
    another operation x32 -> x0, other arithmetic: 35.9 us -> none  [contribute(): pick_left = jnp.argmax(match_left.astype(jnp.int32), axis=2)]
    dynamic_slice x48 -> x0, local copies, waits for them, and re-layouts: 29.9 us -> none  [the longest x16 18.7 us: pick_tile(): vals = lax.dynamic_slice_in_dim(all_vals, start, slot_count, 0)]
  transfers between devices with their start and end apart: 4 -> 0, of which waited for: 1 -> 0; matrix products, arithmetic and copies ran while one was open for 36% -> 0% of each run, Pallas kernels for 0% -> 0%
where the time goes in v1:
time: 114 us; the launch traced here: 112 us
  Pallas kernels  109 us (96%)
  between operations  1.95 us (2%)
  local copies, waits for them, and re-layouts  1.45 us (1%)
    pallas_call x1, Pallas kernels, per_device(): pl.pallas_call(functools.partial(first_gather, rows, cols), out_shape=[ja...  50.7 us
    pallas_call x1, Pallas kernels, per_device(): pl.pallas_call(functools.partial(second_gather, rows, cols), out_shape=[j...  45.5 us
    pallas_call x2, Pallas kernels, products(): pl.pallas_call(functools.partial(block_products, rows, cols, right_lane,...  12.3 us

profile of v1, /device:TPU:0, one launch (start us, length us, event | category | flops | bytes accessed | tf_op | source)
XLA Modules:
  0.0 111.9 jit_solution(5000613046047817632)
XLA Ops:
  1.9 0.8 slice_bitcast_fusion
  2.7 0.1 concatenate.3
  2.8 0.6 broadcast_in_dim.2.meta_ref
  3.4 50.7 %first_gather.1 = (bf16[4,12,128,128]{3,2,1,0:T(8,128)(2,1)}, bf16[8,12,128,128]{3,2,1,0:T(8,128)(2,1)}, s32[4,8,128]{2,1,0:T(8,128)}, s32[8,8,128]{2,1,0:T(8,128)}) custom-call(bf16[12,128,128]{2,1,0:T(8,128)(2,1)} %p_ref.3, bf16[12,128,128]{2,1,0:T(8,128)(2,1)} %h_ref.1, s32[8,128]{1,0:T(8,128)} %broadcast_in_dim.2.meta_ref), custom_call_target="tpu_custom_call" | custom-call | tf_op jit(solution)/shard_map/first_gather/pallas_call | solution.py:346
  54.1 6.3 %products.2 = (bf16[12,128,128]{2,1,0:T(8,128)(2,1)}, f32[8,128]{1,0:T(8,128)}) custom-call(s32[4,8,128]{2,1,0:T(8,128)} %get-tuple-element.14.lmeta, s32[8,8,128]{2,1,0:T(8,128)} %get-tuple-element.15.rmeta, bf16[48,128,128]{2,1,0:T(8,128)(2,1)} %bitcast.20, bf16[96,128,128]{2,1,0:T(8,128)(2,1)} %bitcast.17), custom_call_target="tpu_custom_call" | custom-call | tf_op jit(solution)/shard_map/products/pallas_call | solution.py:364
  60.4 45.5 %second_gather.1 = (bf16[4,12,128,128]{3,2,1,0:T(8,128)(2,1)}, bf16[8,12,128,128]{3,2,1,0:T(8,128)(2,1)}, f32[8,128]{1,0:T(8,128)}) custom-call(bf16[12,128,128]{2,1,0:T(8,128)(2,1)} %p_ref.3, bf16[12,128,128]{2,1,0:T(8,128)(2,1)} %get-tuple-element.11.f_ref, f32[8,128]{1,0:T(8,128)} %get-tuple-element.19.e_ref), custom_call_target="tpu_custom_call" | custom-call | tf_op jit(solution)/shard_map/second_gather/pallas_call | solution.py:396
  106.0 6.0 %products.3 = (bf16[12,128,128]{2,1,0:T(8,128)(2,1)}, f32[1,1]{1,0:T(1,128)}) custom-call(s32[4,8,128]{2,1,0:T(8,128)} %get-tuple-element.14.lmeta, s32[8,8,128]{2,1,0:T(8,128)} %get-tuple-element.15.rmeta, bf16[48,128,128]{2,1,0:T(8,128)(2,1)} %bitcast.19, bf16[96,128,128]{2,1,0:T(8,128)(2,1)} %bitcast.18, f32[8,128]{1,0:T(8,128)} %get-tuple-element.22.rest_0_), custom_call_target="tpu_custom_call" | custom-call | tf_op jit(solution)/shard_map/products/pallas_call | solution.py:364
  (1 shorter events, 0.0 us)

commit v2 on v1

--- a/solution.py
+++ b/solution.py
@@ -8,7 +8,7 @@
 from jax.sharding import PartitionSpec as P
 
 TILE = 8
-CHUNKS = 3
+CHUNKS = 6
 IN_FLIGHT = 16
 MESH = pl.DeviceIdType.MESH
 ANY = pl.BlockSpec(memory_space=pl.ANY)
@@ -50,87 +50,120 @@
 
 
 class ColumnGather:
-    def __init__(self, rows, own, out, own_send, own_recv, fwd_send):
-        self.rows, self.own, self.out = rows, own, out
-        self.sems = own_send, own_recv, fwd_send
+    def __init__(self, rows, own, land, out, up_send, down_send, x_send, recv, local):
+        self.own, self.land, self.out = own, land, out
+        self.up_send, self.down_send, self.x_send = up_send, down_send, x_send
+        self.recv, self.local = recv, local
         self.inner = 2 if rows % 2 == 0 else 1
         self.outer = rows // self.inner
-        slots = own.shape[0]
-        self.chunks = CHUNKS if slots % CHUNKS == 0 else 1
-        self.size = slots // self.chunks
+        self.chunks = recv.shape[1]
+        self.size = own.shape[0] // self.chunks
         self.me = lax.axis_index("row")
         self.x, self.z = self.me % self.inner, self.me // self.inner
-        self.pair = self.z * self.inner + (self.inner - 1 - self.x)
-
-    def row_of(self, d):
-        return ((self.z + d) % self.outer) * self.inner + self.x
+        self.cross_first = 1 if self.inner == 2 and self.chunks > 1 else 0
+
+    def row(self, z, line):
+        return z * self.inner + (self.x if line == 0 else self.inner - 1 - self.x)
 
     def part(self, ch):
         return pl.ds(ch * self.size, self.size)
 
-    def send(self, ch, d):
-        own_send, recv, _ = self.sems
-        target = self.pair if d == 0 else self.row_of(d)
-        return remote(
-            self.own.at[self.part(ch)],
-            self.out.at[self.me, self.part(ch)],
-            own_send.at[d, ch],
-            recv.at[self.me, ch],
-            at_row(target),
-        )
-
-    def forward(self, ch, d):
-        _, recv, fwd = self.sems
-        r = self.row_of(d)
-        return remote(
-            self.out.at[r, self.part(ch)],
-            self.out.at[r, self.part(ch)],
-            fwd.at[d, ch],
-            recv.at[r, ch],
-            at_row(self.pair),
-        )
-
-    def arrival(self, ch, r):
-        _, recv, fwd = self.sems
-        return remote(
-            self.out.at[r, self.part(ch)],
-            self.out.at[r, self.part(ch)],
-            fwd.at[0, ch],
-            recv.at[r, ch],
-            at_row(self.pair),
-        )
-
-    def order(self):
-        out = []
-        for k in range(1, self.outer):
-            d = (k + 1) // 2 if k % 2 else -(k // 2)
-            out.append(d % self.outer)
-        return out
+    def copy(self, r, ch, own, way):
+        sems, target = {
+            "up": (self.up_send, self.me + self.inner),
+            "down": (self.down_send, self.me - self.inner),
+            "x": (self.x_send, self.row(self.z, 1)),
+        }[way]
+        part = self.part(ch)
+        src = self.own.at[part] if own else self.land.at[r, part]
+        return remote(src, self.land.at[r, part], sems.at[r, ch], self.recv.at[r, ch], at_row(target))
+
+    def keep(self, r, ch):
+        part = self.part(ch)
+        return pltpu.make_async_copy(self.land.at[r, part], self.out.at[r, part], self.local.at[r, ch])
+
+    def along(self, r, ch, own, act):
+        @pl.when(self.z < self.outer - 1)
+        def _():
+            act(self.copy(r, ch, own, "up"))
+
+        @pl.when(self.z > 0)
+        def _():
+            act(self.copy(r, ch, own, "down"))
+
+    def arrive(self, r, ch):
+        self.copy(r, ch, False, "x").wait_recv()
+        self.keep(r, ch).start()
 
     def start(self):
         for ch in range(self.chunks):
             if self.inner == 2:
-                self.send(ch, 0).start()
-            for d in self.order():
-                self.send(ch, d).start()
-
-    def relay(self, ch):
-        for d in self.order():
-            self.arrival(ch, self.row_of(d)).wait_recv()
-            if self.inner == 2:
-                self.forward(ch, d).start()
+                self.copy(self.me, ch, True, "x").start()
+            self.along(self.me, ch, True, lambda copy: copy.start())
+        if self.cross_first:
+            r = self.row(self.z, 1)
+            self.arrive(r, 0)
+            self.along(r, 0, False, lambda copy: copy.start())
+
+    def pieces(self):
+        lines = [(ch, 0) for ch in range(self.chunks)]
+        if self.cross_first:
+            lines.insert(1, (0, 1))
+        return lines
+
+    def relayed(self, d, side, ch, line, act):
+        z = self.z - d if side == 0 else self.z + d
+        there = self.z >= d if side == 0 else self.z + d < self.outer
+        r = self.row(z, line)
+
+        @pl.when(there)
+        def _():
+            if act == "start":
+                self.arrive(r, ch)
+            on = self.z < self.outer - 1 if side == 0 else self.z > 0
+
+            @pl.when(on)
+            def _():
+                copy = self.copy(r, ch, False, "up" if side == 0 else "down")
+                copy.start() if act == "start" else copy.wait_send()
+
+            if self.inner == 2 and ch >= self.cross_first:
+                copy = self.copy(r, ch, False, "x")
+                copy.start() if act == "start" else copy.wait_send()
+
+    def relay(self, d):
+        for ch, line in self.pieces():
+            for side in range(2):
+                self.relayed(d, side, ch, line, "start")
 
     def finish(self):
+        if self.inner == 2:
+            for ch in range(self.cross_first, self.chunks):
+                self.arrive(self.row(self.z, 1), ch)
+            for d in range(1, self.outer):
+                for side in range(2):
+                    z = self.z - d if side == 0 else self.z + d
+                    there = self.z >= d if side == 0 else self.z + d < self.outer
+
+                    @pl.when(there)
+                    def _():
+                        for ch in range(self.cross_first, self.chunks):
+                            self.arrive(self.row(z, 1), ch)
         for ch in range(self.chunks):
             if self.inner == 2:
-                self.arrival(ch, self.pair).wait_recv()
-                self.send(ch, 0).wait_send()
-            for d in self.order():
-                self.send(ch, d).wait_send()
-                if self.inner == 2:
-                    other = ((self.z + d) % self.outer) * self.inner + (1 - self.x)
-                    self.arrival(ch, other).wait_recv()
-                    self.forward(ch, d).wait_send()
+                self.copy(self.me, ch, True, "x").wait_send()
+            self.along(self.me, ch, True, lambda copy: copy.wait_send())
+        if self.cross_first:
+            self.along(self.row(self.z, 1), 0, False, lambda copy: copy.wait_send())
+        for d in range(1, self.outer):
+            for ch, line in self.pieces():
+                for side in range(2):
+                    self.relayed(d, side, ch, line, "wait")
+        for r in range(self.inner * self.outer):
+            @pl.when(r != self.me)
+            def _():
+                for ch in range(self.chunks):
+                    self.keep(r, ch).wait()
 
 
 def col_copies(cols, own, out, send, recv):
@@ -155,7 +188,8 @@
 
 def first_gather(
     rows, cols, p_ref, h_ref, meta_ref, prow, hcol, prow_meta, col_meta,
-    own_send, own_recv, fwd_send, p_send, p_recv, mc_send, mc_recv, mr_send, mr_recv, local,
+    land, up_send, down_send, x_send, recv, out_sems,
+    p_send, p_recv, mc_send, mc_recv, mr_send, mr_recv, local,
 ):
     me_row, me_col = lax.axis_index("row"), lax.axis_index("col")
     keep = [
@@ -165,8 +199,9 @@
         pltpu.make_async_copy(meta_ref, col_meta.at[me_row], local.at[3]),
     ]
     greet(rows, cols)
-    gather = ColumnGather(rows, h_ref, hcol, own_send, own_recv, fwd_send)
-    gather.start()
+    gather = ColumnGather(
+        rows, h_ref, land, hcol, up_send, down_send, x_send, recv, out_sems
+    )
     across = (
         col_copies(cols, p_ref, prow, p_send, p_recv)
         + col_copies(cols, meta_ref, prow_meta, mc_send, mc_recv)
@@ -174,8 +209,9 @@
     )
     for copy in across + keep:
         copy.start()
-    for ch in range(gather.chunks):
-        gather.relay(ch)
+    gather.start()
+    for d in range(1, gather.outer):
+        gather.relay(d)
     gather.finish()
     for copy in across + keep:
         copy.wait()
@@ -184,7 +220,8 @@
 def second_gather(
     rows, cols, p_ref, f_ref, e_ref, frow, pcol, e_out,
     e_cols, e_rows, e_sum,
-    own_send, own_recv, fwd_send, p_send, p_recv, ec_send, ec_recv, er_send, er_recv, local,
+    land, up_send, down_send, x_send, recv, out_sems,
+    p_send, p_recv, ec_send, ec_recv, er_send, er_recv, local,
 ):
     me_row, me_col = lax.axis_index("row"), lax.axis_index("col")
     keep = [
@@ -195,11 +232,13 @@
     energies = col_copies(cols, e_ref, e_cols, ec_send, ec_recv)
     for copy in energies:
         copy.start()
-    gather = ColumnGather(rows, p_ref, pcol, own_send, own_recv, fwd_send)
-    gather.start()
+    gather = ColumnGather(
+        rows, p_ref, land, pcol, up_send, down_send, x_send, recv, out_sems
+    )
     across = col_copies(cols, f_ref, frow, p_send, p_recv)
     for copy in across + keep:
         copy.start()
+    gather.start()
     e_cols[me_col] = e_ref[...]
     for copy in energies:
         copy.wait()
@@ -208,12 +247,13 @@
         total = total + e_cols[c]
     e_sum[...] = total
     e_rows[me_row] = total
-    gather.relay(0)
+    if gather.outer > 1:
+        gather.relay(1)
     sums = row_copies(rows, e_sum, e_rows, er_send, er_recv)
     for copy in sums:
         copy.start()
-    for ch in range(1, gather.chunks):
-        gather.relay(ch)
+    for d in range(2, gather.outer):
+        gather.relay(d)
     for copy in sums:
         copy.wait()
     total = e_rows[0]
@@ -339,7 +379,8 @@
     )
     meta = jnp.broadcast_to(jnp.pad(meta, (0, 128 - meta.shape[0]))[None, :], (8, 128))
     dma = pltpu.SemaphoreType.DMA
-    chunk_sems = [dma((rows, CHUNKS)), dma((rows, CHUNKS)), dma((rows, CHUNKS))]
+    chunks = CHUNKS if slots % CHUNKS == 0 else 1
+    chunk_sems = [pltpu.VMEM((rows, slots, size, size), dtype)] + [dma((rows, chunks))] * 5
     col_sems = [dma((cols,)), dma((cols,))]
     row_sems = [dma((rows,)), dma((rows,))]
     tile = (slots, size, size)

time: 114 us -> 104 us (0.912); the launches traced: 112 us -> 105 us
  Pallas kernels: 109 us -> 102 us
    pallas_call x1, Pallas kernels: 50.7 us -> 44.7 us  [per_device(): pl.pallas_call(functools.partial(first_gather, rows, cols), out_shape=[ja...]
    pallas_call x1, Pallas kernels: 45.5 us -> 40.4 us  [per_device(): pl.pallas_call(functools.partial(second_gather, rows, cols), out_shape=[j...]
    pallas_call x2, Pallas kernels: 12.3 us -> 16.6 us  [products(): pl.pallas_call(functools.partial(block_products, rows, cols, right_lane,...]
where the time goes in v2:
time: 104 us; the launch traced here: 105 us
  Pallas kernels  102 us (98%)
  between operations  1.95 us (2%)
  local copies, waits for them, and re-layouts  1.45 us (1%)
    pallas_call x1, Pallas kernels, per_device(): pl.pallas_call(functools.partial(first_gather, rows, cols), out_shape=[ja...  44.7 us
    pallas_call x1, Pallas kernels, per_device(): pl.pallas_call(functools.partial(second_gather, rows, cols), out_shape=[j...  40.4 us
    pallas_call x2, Pallas kernels, products(): pl.pallas_call(functools.partial(block_products, rows, cols, right_lane,...  16.6 us

profile of v2, /device:TPU:0, one launch (start us, length us, event | category | flops | bytes accessed | tf_op | source)
XLA Modules:
  0.0 105.0 jit_solution(8021018031840077788)
XLA Ops:
  1.9 0.8 slice_bitcast_fusion
  2.7 0.1 concatenate.3
  2.8 0.6 broadcast_in_dim.2.meta_ref
  3.4 44.7 %first_gather.1 = (bf16[4,12,128,128]{3,2,1,0:T(8,128)(2,1)}, bf16[8,12,128,128]{3,2,1,0:T(8,128)(2,1)}, s32[4,8,128]{2,1,0:T(8,128)}, s32[8,8,128]{2,1,0:T(8,128)}) custom-call(bf16[12,128,128]{2,1,0:T(8,128)(2,1)} %p_ref.3, bf16[12,128,128]{2,1,0:T(8,128)(2,1)} %h_ref.1, s32[8,128]{1,0:T(8,128)} %broadcast_in_dim.2.meta_ref), custom_call_target="tpu_custom_call" | custom-call | tf_op jit(solution)/shard_map/first_gather/pallas_call | solution.py:387
  48.0 6.7 %products.2 = (bf16[12,128,128]{2,1,0:T(8,128)(2,1)}, f32[8,128]{1,0:T(8,128)}) custom-call(s32[4,8,128]{2,1,0:T(8,128)} %get-tuple-element.14.lmeta, s32[8,8,128]{2,1,0:T(8,128)} %get-tuple-element.15.rmeta, bf16[48,128,128]{2,1,0:T(8,128)(2,1)} %bitcast.20, bf16[96,128,128]{2,1,0:T(8,128)(2,1)} %bitcast.17), custom_call_target="tpu_custom_call" | custom-call | tf_op jit(solution)/shard_map/products/pallas_call | solution.py:405
  54.8 40.4 %second_gather.1 = (bf16[4,12,128,128]{3,2,1,0:T(8,128)(2,1)}, bf16[8,12,128,128]{3,2,1,0:T(8,128)(2,1)}, f32[8,128]{1,0:T(8,128)}) custom-call(bf16[12,128,128]{2,1,0:T(8,128)(2,1)} %p_ref.3, bf16[12,128,128]{2,1,0:T(8,128)(2,1)} %get-tuple-element.11.f_ref, f32[8,128]{1,0:T(8,128)} %get-tuple-element.19.e_ref), custom_call_target="tpu_custom_call" | custom-call | tf_op jit(solution)/shard_map/second_gather/pallas_call | solution.py:437
  95.2 9.8 %products.3 = (bf16[12,128,128]{2,1,0:T(8,128)(2,1)}, f32[1,1]{1,0:T(1,128)}) custom-call(s32[4,8,128]{2,1,0:T(8,128)} %get-tuple-element.14.lmeta, s32[8,8,128]{2,1,0:T(8,128)} %get-tuple-element.15.rmeta, bf16[48,128,128]{2,1,0:T(8,128)(2,1)} %bitcast.19, bf16[96,128,128]{2,1,0:T(8,128)(2,1)} %bitcast.18, f32[8,128]{1,0:T(8,128)} %get-tuple-element.22.rest_0_), custom_call_target="tpu_custom_call" | custom-call | tf_op jit(solution)/shard_map/products/pallas_call | solution.py:405
  (1 shorter events, 0.0 us)

commit v3 on v2

--- a/solution.py
+++ b/solution.py
@@ -62,6 +62,9 @@
         self.x, self.z = self.me % self.inner, self.me // self.inner
         self.cross_first = 1 if self.inner == 2 and self.chunks > 1 else 0
 
+    def later(self, ch):
+        return (ch + self.cross_first) % self.chunks
+
     def row(self, z, line):
         return z * self.inner + (self.x if line == 0 else self.inner - 1 - self.x)
 
@@ -99,17 +102,15 @@
         for ch in range(self.chunks):
             if self.inner == 2:
                 self.copy(self.me, ch, True, "x").start()
-            self.along(self.me, ch, True, lambda copy: copy.start())
+            self.along(self.me, self.later(ch), True, lambda copy: copy.start())
         if self.cross_first:
             r = self.row(self.z, 1)
             self.arrive(r, 0)
             self.along(r, 0, False, lambda copy: copy.start())
 
     def pieces(self):
-        lines = [(ch, 0) for ch in range(self.chunks)]
-        if self.cross_first:
-            lines.insert(1, (0, 1))
-        return lines
+        lines = [(self.later(ch), 0) for ch in range(self.chunks)]
+        return lines + [(0, 1)] * self.cross_first
 
     def relayed(self, d, side, ch, line, act):
         z = self.z - d if side == 0 else self.z + d
@@ -281,17 +282,17 @@
     count_lane = 4 * slots
     acc[...] = jnp.zeros_like(acc)
 
-    for t in range(TILE):
+    for t in range(TILE + 1):
         head[t] = -1
 
-    for t in range(tile_cols * words):
+    for t in range(tile_cols * words + 1):
         mask[t] = 0
 
     @pl.loop(0, cols)
     def _(c):
-        @pl.loop(0, lmeta[c, 0, count_lane])
-        def _(s):
-            row = lmeta[c, 0, s] - i * TILE
+        live = lmeta[c, 0, count_lane]
+        for s in range(slots):
+            row = jnp.where(s < live, lmeta[c, 0, s] - i * TILE, TILE)
             idx = c * slots + s
             inner[idx] = lmeta[c, 0, slots + s]
             nxt[idx] = head[row]
@@ -299,13 +300,13 @@
 
     @pl.loop(0, rows)
     def _(r):
-        @pl.loop(0, rmeta[r, 0, count_lane + (1 if right_lane else 0)])
-        def _(s):
+        live = rmeta[r, 0, count_lane + (1 if right_lane else 0)]
+        for s in range(slots):
             k = rmeta[r, 0, right_lane + s]
             col = rmeta[r, 0, right_lane + slots + s] - j * tile_cols
-            word = col * words + (k >> 5)
+            word = jnp.where(s < live, col * words + (k >> 5), tile_cols * words)
             mask[word] = mask[word] | (jnp.int32(1) << (k & 31))
-            table[k * tile_cols + col] = r * slots + s
+            table[jnp.where(s < live, k * tile_cols + col, nblk * tile_cols)] = r * slots + s
 
     def find_slot(s, n):
         row = lmeta[j, 0, s] - i * TILE
@@ -414,11 +415,11 @@
                 pltpu.VMEM(tile, jnp.float32),
                 pltpu.VMEM((IN_FLIGHT, size, size), dtype),
                 pltpu.VMEM((IN_FLIGHT, size, size), dtype),
-                smem(TILE),
+                smem(TILE + 1),
                 smem(cols * slots),
                 smem(cols * slots),
-                smem(tile_cols * words),
-                smem(nblk * tile_cols),
+                smem(tile_cols * words + 1),
+                smem(nblk * tile_cols + 1),
                 smem(most),
                 smem(most),
                 smem(most),

time: 104 us -> 96.5 us (0.928); the launches traced: 105 us -> 96.2 us
  Pallas kernels: 102 us -> 92.8 us
    pallas_call x2, Pallas kernels: 16.6 us -> 10.8 us  [products(): pl.pallas_call(functools.partial(block_products, rows, cols, right_lane,...]
    pallas_call x1, Pallas kernels: 44.7 us -> 42.3 us  [per_device(): pl.pallas_call(functools.partial(first_gather, rows, cols), out_shape=[ja...]
where the time goes in v3:
time: 96.5 us; the launch traced here: 96.2 us
  Pallas kernels  92.8 us (96%)
  between operations  1.95 us (2%)
  local copies, waits for them, and re-layouts  1.45 us (2%)
    pallas_call x1, Pallas kernels, per_device(): pl.pallas_call(functools.partial(first_gather, rows, cols), out_shape=[ja...  42.3 us
    pallas_call x1, Pallas kernels, per_device(): pl.pallas_call(functools.partial(second_gather, rows, cols), out_shape=[j...  39.7 us
    pallas_call x2, Pallas kernels, products(): pl.pallas_call(functools.partial(block_products, rows, cols, right_lane,...  10.8 us

profile of v3, /device:TPU:0, one launch (start us, length us, event | category | flops | bytes accessed | tf_op | source)
XLA Modules:
  0.0 96.2 jit_solution(5317505110913825386)
XLA Ops:
  1.9 0.8 slice_bitcast_fusion
  2.7 0.1 concatenate.3
  2.8 0.6 broadcast_in_dim.2.meta_ref
  3.4 42.3 %first_gather.1 = (bf16[4,12,128,128]{3,2,1,0:T(8,128)(2,1)}, bf16[8,12,128,128]{3,2,1,0:T(8,128)(2,1)}, s32[4,8,128]{2,1,0:T(8,128)}, s32[8,8,128]{2,1,0:T(8,128)}) custom-call(bf16[12,128,128]{2,1,0:T(8,128)(2,1)} %p_ref.3, bf16[12,128,128]{2,1,0:T(8,128)(2,1)} %h_ref.1, s32[8,128]{1,0:T(8,128)} %broadcast_in_dim.2.meta_ref), custom_call_target="tpu_custom_call" | custom-call | tf_op jit(solution)/shard_map/first_gather/pallas_call | solution.py:388
  45.7 5.2 %products.2 = (bf16[12,128,128]{2,1,0:T(8,128)(2,1)}, f32[8,128]{1,0:T(8,128)}) custom-call(s32[4,8,128]{2,1,0:T(8,128)} %get-tuple-element.14.lmeta, s32[8,8,128]{2,1,0:T(8,128)} %get-tuple-element.15.rmeta, bf16[48,128,128]{2,1,0:T(8,128)(2,1)} %bitcast.20, bf16[96,128,128]{2,1,0:T(8,128)(2,1)} %bitcast.17), custom_call_target="tpu_custom_call" | custom-call | tf_op jit(solution)/shard_map/products/pallas_call | solution.py:406
  50.8 39.7 %second_gather.1 = (bf16[4,12,128,128]{3,2,1,0:T(8,128)(2,1)}, bf16[8,12,128,128]{3,2,1,0:T(8,128)(2,1)}, f32[8,128]{1,0:T(8,128)}) custom-call(bf16[12,128,128]{2,1,0:T(8,128)(2,1)} %p_ref.3, bf16[12,128,128]{2,1,0:T(8,128)(2,1)} %get-tuple-element.11.f_ref, f32[8,128]{1,0:T(8,128)} %get-tuple-element.19.e_ref), custom_call_target="tpu_custom_call" | custom-call | tf_op jit(solution)/shard_map/second_gather/pallas_call | solution.py:438
  90.5 5.6 %products.3 = (bf16[12,128,128]{2,1,0:T(8,128)(2,1)}, f32[1,1]{1,0:T(1,128)}) custom-call(s32[4,8,128]{2,1,0:T(8,128)} %get-tuple-element.14.lmeta, s32[8,8,128]{2,1,0:T(8,128)} %get-tuple-element.15.rmeta, bf16[48,128,128]{2,1,0:T(8,128)(2,1)} %bitcast.19, bf16[96,128,128]{2,1,0:T(8,128)(2,1)} %bitcast.18, f32[8,128]{1,0:T(8,128)} %get-tuple-element.22.rest_0_), custom_call_target="tpu_custom_call" | custom-call | tf_op jit(solution)/shard_map/products/pallas_call | solution.py:406
  (1 shorter events, 0.0 us)

commit v4 on v3

--- a/solution.py
+++ b/solution.py
@@ -8,7 +8,7 @@
 from jax.sharding import PartitionSpec as P
 
 TILE = 8
-CHUNKS = 6
+CHUNKS = 12
 IN_FLIGHT = 16
 MESH = pl.DeviceIdType.MESH
 ANY = pl.BlockSpec(memory_space=pl.ANY)
@@ -60,7 +60,7 @@
         self.size = own.shape[0] // self.chunks
         self.me = lax.axis_index("row")
         self.x, self.z = self.me % self.inner, self.me // self.inner
-        self.cross_first = 1 if self.inner == 2 and self.chunks > 1 else 0
+        self.cross_first = self.chunks // 6 if self.inner == 2 else 0
 
     def later(self, ch):
         return (ch + self.cross_first) % self.chunks
@@ -103,14 +103,14 @@
             if self.inner == 2:
                 self.copy(self.me, ch, True, "x").start()
             self.along(self.me, self.later(ch), True, lambda copy: copy.start())
-        if self.cross_first:
+        for ch in range(self.cross_first):
             r = self.row(self.z, 1)
-            self.arrive(r, 0)
-            self.along(r, 0, False, lambda copy: copy.start())
+            self.arrive(r, ch)
+            self.along(r, ch, False, lambda copy: copy.start())
 
     def pieces(self):
         lines = [(self.later(ch), 0) for ch in range(self.chunks)]
-        return lines + [(0, 1)] * self.cross_first
+        return lines + [(ch, 1) for ch in range(self.cross_first)]
 
     def relayed(self, d, side, ch, line, act):
         z = self.z - d if side == 0 else self.z + d
@@ -154,8 +154,8 @@
             if self.inner == 2:
                 self.copy(self.me, ch, True, "x").wait_send()
             self.along(self.me, ch, True, lambda copy: copy.wait_send())
-        if self.cross_first:
-            self.along(self.row(self.z, 1), 0, False, lambda copy: copy.wait_send())
+        for ch in range(self.cross_first):
+            self.along(self.row(self.z, 1), ch, False, lambda copy: copy.wait_send())
         for d in range(1, self.outer):
             for ch, line in self.pieces():
                 for side in range(2):

time: 96.5 us -> 100 us (1.036)
  Pallas kernels: 92.8 us -> 96.7 us
    pallas_call x1, Pallas kernels: 39.7 us -> 41.8 us  [per_device(): pl.pallas_call(functools.partial(second_gather, rows, cols), out_shape=[j...]
    pallas_call x1, Pallas kernels: 42.3 us -> 44.1 us  [per_device(): pl.pallas_call(functools.partial(first_gather, rows, cols), out_shape=[ja...]
where the time goes in v4:
time: 100 us
  Pallas kernels  96.7 us (97%)
  between operations  1.95 us (2%)
  local copies, waits for them, and re-layouts  1.45 us (1%)
    pallas_call x1, Pallas kernels, per_device(): pl.pallas_call(functools.partial(first_gather, rows, cols), out_shape=[ja...  44.1 us
    pallas_call x1, Pallas kernels, per_device(): pl.pallas_call(functools.partial(second_gather, rows, cols), out_shape=[j...  41.8 us
    pallas_call x2, Pallas kernels, products(): pl.pallas_call(functools.partial(block_products, rows, cols, right_lane,...  10.8 us

profile of v4, /device:TPU:0, one launch (start us, length us, event | category | flops | bytes accessed | tf_op | source)
XLA Modules:
  0.0 100.1 jit_solution(6835216153313993768)
XLA Ops:
  1.9 0.8 slice_bitcast_fusion
  2.7 0.1 concatenate.3
  2.8 0.6 broadcast_in_dim.2.meta_ref
  3.4 44.1 %first_gather.1 = (bf16[4,12,128,128]{3,2,1,0:T(8,128)(2,1)}, bf16[8,12,128,128]{3,2,1,0:T(8,128)(2,1)}, s32[4,8,128]{2,1,0:T(8,128)}, s32[8,8,128]{2,1,0:T(8,128)}) custom-call(bf16[12,128,128]{2,1,0:T(8,128)(2,1)} %p_ref.3, bf16[12,128,128]{2,1,0:T(8,128)(2,1)} %h_ref.1, s32[8,128]{1,0:T(8,128)} %broadcast_in_dim.2.meta_ref), custom_call_target="tpu_custom_call" | custom-call | tf_op jit(solution)/shard_map/first_gather/pallas_call | solution.py:388
  47.5 5.3 %products.2 = (bf16[12,128,128]{2,1,0:T(8,128)(2,1)}, f32[8,128]{1,0:T(8,128)}) custom-call(s32[4,8,128]{2,1,0:T(8,128)} %get-tuple-element.14.lmeta, s32[8,8,128]{2,1,0:T(8,128)} %get-tuple-element.15.rmeta, bf16[48,128,128]{2,1,0:T(8,128)(2,1)} %bitcast.20, bf16[96,128,128]{2,1,0:T(8,128)(2,1)} %bitcast.17), custom_call_target="tpu_custom_call" | custom-call | tf_op jit(solution)/shard_map/products/pallas_call | solution.py:406
  52.8 41.8 %second_gather.1 = (bf16[4,12,128,128]{3,2,1,0:T(8,128)(2,1)}, bf16[8,12,128,128]{3,2,1,0:T(8,128)(2,1)}, f32[8,128]{1,0:T(8,128)}) custom-call(bf16[12,128,128]{2,1,0:T(8,128)(2,1)} %p_ref.3, bf16[12,128,128]{2,1,0:T(8,128)(2,1)} %get-tuple-element.11.f_ref, f32[8,128]{1,0:T(8,128)} %get-tuple-element.19.e_ref), custom_call_target="tpu_custom_call" | custom-call | tf_op jit(solution)/shard_map/second_gather/pallas_call | solution.py:438
  94.6 5.5 %products.3 = (bf16[12,128,128]{2,1,0:T(8,128)(2,1)}, f32[1,1]{1,0:T(1,128)}) custom-call(s32[4,8,128]{2,1,0:T(8,128)} %get-tuple-element.14.lmeta, s32[8,8,128]{2,1,0:T(8,128)} %get-tuple-element.15.rmeta, bf16[48,128,128]{2,1,0:T(8,128)(2,1)} %bitcast.19, bf16[96,128,128]{2,1,0:T(8,128)(2,1)} %bitcast.18, f32[8,128]{1,0:T(8,128)} %get-tuple-element.22.rest_0_), custom_call_target="tpu_custom_call" | custom-call | tf_op jit(solution)/shard_map/products/pallas_call | solution.py:406
  (1 shorter events, 0.0 us)
